TPU v7x, 32 devices: a whole 2x2x4 slice. The times are simulated.
32 devices in a mesh: row: 8 (over z, core), col: 4 (over y, x).
Axes of the slice: x: 2, y: 2, z: 4, core: 2. Of those that a mesh axis runs over, the one named last changes fastest.
Arguments:
- right_sides: float32 [4, 1024, 4096], P(None, 'row', 'col'), may hold values from -6 to 6
- low_left: bfloat16 [6, 4096, 128], P(None, 'col'), may hold values from -0.25 to 0.25
- low_right: bfloat16 [6, 4096, 128], P(None, 'col'), may hold values from -0.09375 to 0.09375
- up_left: bfloat16 [6, 4096, 128], P(None, 'col'), may hold values from -0.25 to 0.25
- up_right: bfloat16 [6, 4096, 128], P(None, 'col'), may hold values from -0.09375 to 0.09375
- low_ranks: int32 [6], replicated, may hold values from 1 to 4
- up_ranks: int32 [6], replicated, may hold values from 1 to 4
- inv_lower: bfloat16 [4, 4096, 4096], P(None, 'col', 'row'), may hold values from -0.09375 to 0.09375
- inv_upper: bfloat16 [4, 4096, 4096], P(None, 'col', 'row'), may hold values from -0.09375 to 0.09375
Outputs:
- solution: float32 [4, 1024, 4096], P(None, 'row', 'col')
Inputs may be any that keep to these rules, and one draw needn't show every extreme that they name: `low_ranks`: factor columns beyond 32 times this value are padding with arbitrary values and must be masked out. `up_ranks`: factor columns beyond 32 times this value are padding with arbitrary values and must be masked out.
All inputs are finite; a program needn't handle non-finite values.
Results may differ from a plain program's by a relative error of at most 0.03.
Values may be sent and summed in bfloat16 or wider, within the bound.
A program may use at most 64 MiB of HBM per device.

v0:
```python
import jax
import jax.numpy as jnp
import numpy as np
from jax import lax
from jax.sharding import PartitionSpec as P

RBLK = 32


def rank_mask(ranks, pair_index, rank_cols):
    columns = jnp.arange(rank_cols, dtype=jnp.int32)
    return (columns[None, :] < RBLK * ranks[pair_index][:, None]).astype(jnp.float32)


def times_inverse(block, inverse):
    return lax.dot_general(
        block, inverse, (((1,), (1,)), ((), ())), preferred_element_type=jnp.float32
    )


def sum_terms(moved, inverse):
    return times_inverse(moved, inverse)


def shards(
    right_sides, low_left, low_right, up_left, up_right, low_ranks, up_ranks, inv_lower, inv_upper
):
    tile_count = right_sides.shape[0]
    rank_cols = low_left.shape[2]
    residual = right_sides
    forward = []
    for section in range(tile_count):
        rounded = residual[section].astype(jnp.bfloat16)
        whole = lax.all_gather(rounded, "col", axis=1, tiled=True)
        moved = lax.all_to_all(whole, "row", split_axis=1, concat_axis=0, tiled=True)
        solved = lax.psum_scatter(
            sum_terms(moved, inv_lower[section]).astype(jnp.bfloat16),
            "row",
            scatter_dimension=0,
            tiled=True,
        ).astype(jnp.float32)
        forward.append(solved)
        if section + 1 < tile_count:
            pair_index = np.array(
                [tile * (tile - 1) // 2 + section for tile in range(section + 1, tile_count)],
                dtype=np.int32,
            )
            projections = jnp.einsum(
                "nw,mwr->mnr",
                solved.astype(jnp.bfloat16),
                low_right[pair_index],
                preferred_element_type=jnp.float32,
            )
            leading = lax.psum(projections[:1].astype(jnp.bfloat16), "col").astype(jnp.float32)
            if section + 2 < tile_count:
                remaining = lax.psum(projections[1:].astype(jnp.bfloat16), "col").astype(
                    jnp.float32
                )
                summed = jnp.concatenate([leading, remaining], axis=0)
            else:
                summed = leading
            masked = (summed * rank_mask(low_ranks, pair_index, rank_cols)[:, None, :]).astype(
                jnp.bfloat16
            )
            update = jnp.einsum(
                "mnr,mwr->mnw", masked, low_left[pair_index], preferred_element_type=jnp.float32
            )
            residual = residual.at[section + 1 :].add(-update)
    state = jnp.stack(forward)
    solutions = [None] * tile_count
    for section in range(tile_count - 1, -1, -1):
        rounded = state[section].astype(jnp.bfloat16)
        whole = lax.all_gather(rounded, "col", axis=1, tiled=True)
        moved = lax.all_to_all(whole, "row", split_axis=1, concat_axis=0, tiled=True)
        solved = lax.psum_scatter(
            sum_terms(moved, inv_upper[section]).astype(jnp.bfloat16),
            "row",
            scatter_dimension=0,
            tiled=True,
        ).astype(jnp.float32)
        solutions[section] = solved
        if section > 0:
            pair_index = np.array(
                [section * (section - 1) // 2 + tile for tile in range(section)], dtype=np.int32
            )
            projections = jnp.einsum(
                "nw,mwr->mnr",
                solved.astype(jnp.bfloat16),
                up_right[pair_index],
                preferred_element_type=jnp.float32,
            )
            leading = lax.psum(projections[-1:].astype(jnp.bfloat16), "col").astype(jnp.float32)
            if section > 1:
                remaining = lax.psum(projections[:-1].astype(jnp.bfloat16), "col").astype(
                    jnp.float32
                )
                summed = jnp.concatenate([remaining, leading], axis=0)
            else:
                summed = leading
            masked = (summed * rank_mask(up_ranks, pair_index, rank_cols)[:, None, :]).astype(
                jnp.bfloat16
            )
            update = jnp.einsum(
                "mnr,mwr->mnw", masked, up_left[pair_index], preferred_element_type=jnp.float32
            )
            state = state.at[:section].add(-update)
    return jnp.stack(solutions)


def solution(mesh):
    in_specs = (
        P(None, "row", "col"),
        P(None, "col", None),
        P(None, "col", None),
        P(None, "col", None),
        P(None, "col", None),
        P(),
        P(),
        P(None, "col", "row"),
        P(None, "col", "row"),
    )
    out_specs = P(None, "row", "col")
    return jax.shard_map(shards, mesh=mesh, in_specs=in_specs, out_specs=out_specs, check_vma=False)
```

profile of v0, /device:TPU:0, one launch (start us, length us, event | category | flops | bytes accessed | tf_op | source)
XLA Modules:
  0.0 1013.5 jit_solution(5519528377490401830)
XLA Ops:
  8.5 29.9 %all-gather.18.cloned.1.call-done = bf16[1,128,4096]{1,2,0:T(8,128)(2,1)} async-done(((bf16[1,128,1024]{1,2,0:T(8,128)(2,1)}), bf16[1,128,4096]{1,2,0:T(8,128)(2,1)}) %all-gather.18.cloned.1.call-update) | async-done | bytes 1048592 | tf_op jit(solution)/shard_map/all_gather | solution.py:34
  38.4 31.2 %all_to_all.152 = bf16[128,8,512]{0,2,1:T(8,128)(2,1)S(1)} all-to-all(bf16[128,8,512]{0,2,1:T(8,128)(2,1)} %bitcast.171), channel_id=1, replica_groups=mesh['row'=8,'col'=4] {'row'}, dimensions={1} | all-to-all | bytes 2097152 | tf_op jit(solution)/shard_map/all_to_all | solution.py:35
  70.1 3.8 convolution_convert_fusion.7
  76.8 31.4 %reduce-scatter.9.cloned.1.call-done = bf16[128,1024]{1,0:T(8,128)(2,1)} async-done(((bf16[1024,1024]{1,0:T(8,128)(2,1)}), bf16[128,1024]{1,0:T(8,128)(2,1)}) %reduce-scatter.9.cloned.1.call-update) | async-done | bytes 262160 | tf_op jit(solution)/shard_map/reduce_scatter | solution.py:36
  111.1 16.1 %psum.70 = bf16[1,128,128]{1,2,0:T(8,128)(2,1)S(1)} all-reduce(bf16[1,128,128]{1,2,0:T(8,128)(2,1)S(1)} %slice.332), channel_id=1, replica_groups=mesh['row'=8,'col'=4] {'col'}, use_global_device_ids=true, to_apply=%region_1.0 | all-reduce | flops 16384 | bytes 65536 | tf_op jit(solution)/shard_map/psum | solution.py:54
  127.2 24.3 %all-reduce.7.cloned.1.call-done = bf16[2,128,128]{1,2,0:T(8,128)(2,1)} async-done(((bf16[2,128,128]{1,2,0:T(8,128)(2,1)}), bf16[2,128,128]{1,2,0:T(8,128)(2,1)}) %all-reduce.7.cloned.1.call-update) | async-done | bytes 65552 | tf_op jit(solution)/shard_map/psum | solution.py:56
  151.5 2.0 negate_add_fusion.1
  154.2 26.6 %all-gather.20.cloned.1.call-done = bf16[1,128,4096]{2,1,0:T(8,128)(2,1)} async-done(((bf16[1,128,1024]{2,1,0:T(8,128)(2,1)}), bf16[1,128,4096]{2,1,0:T(8,128)(2,1)}) %all-gather.20.cloned.1.call-update) | async-done | bytes 1048592 | tf_op jit(solution)/shard_map/all_gather | solution.py:34
  182.8 31.0 %all_to_all.153 = bf16[128,8,512]{2,0,1:T(8,128)(2,1)S(1)} all-to-all(bf16[128,8,512]{2,0,1:T(8,128)(2,1)S(1)} %copy.61), channel_id=1, replica_groups=mesh['row'=8,'col'=4] {'row'}, dimensions={1} | all-to-all | bytes 2097152 | tf_op jit(solution)/shard_map/all_to_all | solution.py:35
  213.8 3.8 convolution_convert_fusion.6
  218.2 2.1 gather_fusion.3
  220.9 30.8 %reduce-scatter.11.cloned.1.call-done = bf16[128,1024]{1,0:T(8,128)(2,1)} async-done(((bf16[1024,1024]{1,0:T(8,128)(2,1)}), bf16[128,1024]{1,0:T(8,128)(2,1)}) %reduce-scatter.11.cloned.1.call-update) | async-done | bytes 262160 | tf_op jit(solution)/shard_map/reduce_scatter | solution.py:36
  253.9 2.1 gather_fusion.5
  255.9 39.0 %all-reduce.13.cloned.1.call-done = (bf16[1,128,128]{1,2,0:T(8,128)(2,1)}, bf16[1,128,128]{1,2,0:T(8,128)(2,1)}) async-done(((bf16[1,128,128]{1,2,0:T(8,128)(2,1)}, bf16[1,128,128]{1,2,0:T(8,128)(2,1)}), (bf16[1,128,128]{1,2,0:T(8,128)(2,1)}, bf16[1,128,128]{1,2,0:T(8,128)(2,1)})) %all-reduce.13.cloned.1.call-update) | async-done | bytes 65552 | tf_op jit(solution)/shard_map/psum | solution.py:56
  297.0 26.6 %all-gather.22.cloned.1.call-done = bf16[1,128,4096]{2,1,0:T(8,128)(2,1)} async-done(((bf16[1,128,1024]{2,1,0:T(8,128)(2,1)}), bf16[1,128,4096]{2,1,0:T(8,128)(2,1)}) %all-gather.22.cloned.1.call-update) | async-done | bytes 1048592 | tf_op jit(solution)/shard_map/all_gather | solution.py:34
  325.5 31.0 %all_to_all.154 = bf16[128,8,512]{2,0,1:T(8,128)(2,1)S(1)} all-to-all(bf16[128,8,512]{2,0,1:T(8,128)(2,1)S(1)} %copy.64), channel_id=1, replica_groups=mesh['row'=8,'col'=4] {'row'}, dimensions={1} | all-to-all | bytes 2097152 | tf_op jit(solution)/shard_map/all_to_all | solution.py:35
  356.5 3.8 convolution_convert_fusion.5
  361.6 32.9 %reduce-scatter.13.cloned.1.call-done = bf16[128,1024]{1,0:T(8,128)(2,1)} async-done(((bf16[1024,1024]{1,0:T(8,128)(2,1)}), bf16[128,1024]{1,0:T(8,128)(2,1)}) %reduce-scatter.13.cloned.1.call-update) | async-done | bytes 262160 | tf_op jit(solution)/shard_map/reduce_scatter | solution.py:36
  395.8 16.2 %psum.74 = bf16[1,128,128]{2,1,0:T(8,128)(2,1)S(1)} all-reduce(bf16[1,128,128]{2,1,0:T(8,128)(2,1)S(1)} %fusion.12), channel_id=1, replica_groups=mesh['row'=8,'col'=4] {'col'}, use_global_device_ids=true, to_apply=%region_7.0 | all-reduce | flops 16384 | bytes 65536 | tf_op jit(solution)/shard_map/psum | solution.py:54
  412.0 1.9 fusion.7
  414.0 23.0 %all-gather.24.cloned.1.call-done = bf16[1,128,4096]{2,1,0:T(8,128)(2,1)} async-done(((bf16[1,128,1024]{2,1,0:T(8,128)(2,1)}), bf16[1,128,4096]{2,1,0:T(8,128)(2,1)}) %all-gather.24.cloned.1.call-update) | async-done | bytes 1048592 | tf_op jit(solution)/shard_map/all_gather | solution.py:34
  438.9 31.0 %all_to_all.155 = bf16[128,8,512]{2,0,1:T(8,128)(2,1)S(1)} all-to-all(bf16[128,8,512]{2,0,1:T(8,128)(2,1)S(1)} %copy.65), channel_id=1, replica_groups=mesh['row'=8,'col'=4] {'row'}, dimensions={1} | all-to-all | bytes 2097152 | tf_op jit(solution)/shard_map/all_to_all | solution.py:35
  469.9 3.8 convolution_convert_fusion.4
  473.8 34.1 %reduce-scatter.15.cloned.1.call-done = bf16[128,1024]{1,0:T(8,128)(2,1)} async-done(((bf16[1024,1024]{1,0:T(8,128)(2,1)}), bf16[128,1024]{1,0:T(8,128)(2,1)}) %reduce-scatter.15.cloned.1.call-update) | async-done | bytes 262160 | tf_op jit(solution)/shard_map/reduce_scatter | solution.py:36
  508.0 26.8 %all-gather.16.cloned.1.call-done = bf16[128,4096]{1,0:T(8,128)(2,1)} async-done(((bf16[128,1024]{1,0:T(8,128)(2,1)}), bf16[128,4096]{1,0:T(8,128)(2,1)}) %all-gather.16.cloned.1.call-update) | async-done | bytes 1048592 | tf_op jit(solution)/shard_map/all_gather | solution.py:73
  536.1 31.0 %all_to_all.156 = bf16[128,8,512]{2,0,1:T(8,128)(2,1)S(1)} all-to-all(bf16[128,8,512]{2,0,1:T(8,128)(2,1)S(1)} %bitcast.165), channel_id=1, replica_groups=mesh['row'=8,'col'=4] {'row'}, dimensions={1} | all-to-all | bytes 2097152 | tf_op jit(solution)/shard_map/all_to_all | solution.py:74
  567.1 3.8 convolution_convert_fusion.3
  573.8 31.4 %reduce-scatter.17.cloned.1.call-done = bf16[128,1024]{1,0:T(8,128)(2,1)} async-done(((bf16[1024,1024]{1,0:T(8,128)(2,1)}), bf16[128,1024]{1,0:T(8,128)(2,1)}) %reduce-scatter.17.cloned.1.call-update) | async-done | bytes 262160 | tf_op jit(solution)/shard_map/reduce_scatter | solution.py:75
  608.0 16.3 %psum.76 = bf16[1,128,128]{1,2,0:T(8,128)(2,1)S(1)} all-reduce(bf16[1,128,128]{1,2,0:T(8,128)(2,1)S(1)} %slice.341), channel_id=1, replica_groups=mesh['row'=8,'col'=4] {'col'}, use_global_device_ids=true, to_apply=%region_11.0 | all-reduce | flops 16384 | bytes 65536 | tf_op jit(solution)/shard_map/psum | solution.py:92
  624.3 24.1 %all-reduce.9.cloned.1.call-done = bf16[2,128,128]{1,2,0:T(8,128)(2,1)} async-done(((bf16[2,128,128]{1,2,0:T(8,128)(2,1)}), bf16[2,128,128]{1,2,0:T(8,128)(2,1)}) %all-reduce.9.cloned.1.call-update) | async-done | bytes 65552 | tf_op jit(solution)/shard_map/psum | solution.py:94
  650.6 26.6 %all-gather.26.cloned.1.call-done = bf16[1,128,4096]{2,1,0:T(8,128)(2,1)} async-done(((bf16[1,128,1024]{2,1,0:T(8,128)(2,1)}), bf16[1,128,4096]{2,1,0:T(8,128)(2,1)}) %all-gather.26.cloned.1.call-update) | async-done | bytes 1048592 | tf_op jit(solution)/shard_map/all_gather | solution.py:73
  679.1 31.0 %all_to_all.157 = bf16[128,8,512]{2,0,1:T(8,128)(2,1)S(1)} all-to-all(bf16[128,8,512]{2,0,1:T(8,128)(2,1)S(1)} %copy.69), channel_id=1, replica_groups=mesh['row'=8,'col'=4] {'row'}, dimensions={1} | all-to-all | bytes 2097152 | tf_op jit(solution)/shard_map/all_to_all | solution.py:74
  710.1 3.8 convolution_convert_fusion.2
  714.6 2.1 gather_fusion.9
  717.3 30.9 %reduce-scatter.19.cloned.1.call-done = bf16[128,1024]{1,0:T(8,128)(2,1)} async-done(((bf16[1024,1024]{1,0:T(8,128)(2,1)}), bf16[128,1024]{1,0:T(8,128)(2,1)}) %reduce-scatter.19.cloned.1.call-update) | async-done | bytes 262160 | tf_op jit(solution)/shard_map/reduce_scatter | solution.py:75
  750.2 2.1 gather_fusion.11
  752.3 39.0 %all-reduce.11.cloned.1.call-done = (bf16[1,128,128]{1,2,0:T(8,128)(2,1)}, bf16[1,128,128]{1,2,0:T(8,128)(2,1)}) async-done(((bf16[1,128,128]{1,2,0:T(8,128)(2,1)}, bf16[1,128,128]{1,2,0:T(8,128)(2,1)}), (bf16[1,128,128]{1,2,0:T(8,128)(2,1)}, bf16[1,128,128]{1,2,0:T(8,128)(2,1)})) %all-reduce.11.cloned.1.call-update) | async-done | bytes 65552 | tf_op jit(solution)/shard_map/psum | solution.py:92
  793.3 26.6 %all-gather.28.cloned.1.call-done = bf16[1,128,4096]{2,1,0:T(8,128)(2,1)} async-done(((bf16[1,128,1024]{2,1,0:T(8,128)(2,1)}), bf16[1,128,4096]{2,1,0:T(8,128)(2,1)}) %all-gather.28.cloned.1.call-update) | async-done | bytes 1048592 | tf_op jit(solution)/shard_map/all_gather | solution.py:73
  821.8 31.0 %all_to_all.158 = bf16[128,8,512]{2,0,1:T(8,128)(2,1)S(1)} all-to-all(bf16[128,8,512]{2,0,1:T(8,128)(2,1)S(1)} %copy.72), channel_id=1, replica_groups=mesh['row'=8,'col'=4] {'row'}, dimensions={1} | all-to-all | bytes 2097152 | tf_op jit(solution)/shard_map/all_to_all | solution.py:74
  852.8 3.8 convolution_convert_fusion.1
  856.7 34.1 %reduce-scatter.21.cloned.1.call-done = bf16[128,1024]{1,0:T(8,128)(2,1)} async-done(((bf16[1024,1024]{1,0:T(8,128)(2,1)}), bf16[128,1024]{1,0:T(8,128)(2,1)}) %reduce-scatter.21.cloned.1.call-update) | async-done | bytes 262160 | tf_op jit(solution)/shard_map/reduce_scatter | solution.py:75
  892.0 16.2 %psum.79 = bf16[1,128,128]{2,1,0:T(8,128)(2,1)S(1)} all-reduce(bf16[1,128,128]{2,1,0:T(8,128)(2,1)S(1)} %fusion.13), channel_id=1, replica_groups=mesh['row'=8,'col'=4] {'col'}, use_global_device_ids=true, to_apply=%region_16.0 | all-reduce | flops 16384 | bytes 65536 | tf_op jit(solution)/shard_map/psum | solution.py:92
  908.2 1.9 fusion.6
  910.2 23.0 %all-gather.30.cloned.1.call-done = bf16[1,128,4096]{2,1,0:T(8,128)(2,1)} async-done(((bf16[1,128,1024]{2,1,0:T(8,128)(2,1)}), bf16[1,128,4096]{2,1,0:T(8,128)(2,1)}) %all-gather.30.cloned.1.call-update) | async-done | bytes 1048592 | tf_op jit(solution)/shard_map/all_gather | solution.py:73
  935.1 31.0 %all_to_all.159 = bf16[128,8,512]{2,0,1:T(8,128)(2,1)S(1)} all-to-all(bf16[128,8,512]{2,0,1:T(8,128)(2,1)S(1)} %copy.73), channel_id=1, replica_groups=mesh['row'=8,'col'=4] {'row'}, dimensions={1} | all-to-all | bytes 2097152 | tf_op jit(solution)/shard_map/all_to_all | solution.py:74
  966.1 3.8 convolution_convert_fusion
  970.0 34.2 %reduce-scatter.23.cloned.1.call-done = bf16[128,1024]{1,0:T(8,128)(2,1)} async-done(((bf16[1024,1024]{1,0:T(8,128)(2,1)}), bf16[128,1024]{1,0:T(8,128)(2,1)}) %reduce-scatter.23.cloned.1.call-update) | async-done | bytes 262160 | tf_op jit(solution)/shard_map/reduce_scatter | solution.py:75
  1004.2 2.4 maximum_convert_fusion
  (130 shorter events, 43.7 us)
Async XLA Ops:
  6.5 31.9 %all-gather.18.cloned.1.call-start = ((), (), s32[]{:S(2)}) async-start(), calls=%async_computation.27 | async-start | bytes 1310720 | tf_op jit(solution)/shard_map/all_gather | solution.py:34
  8.5 99.7 %reduce-scatter.9.cloned.1.call-start = ((), (), s32[]{:S(2)}) async-start(), calls=%async_computation.16 | async-start | bytes 2359296 | tf_op jit(solution)/shard_map/reduce_scatter | solution.py:36
  74.0 0.7 copy-start.15
  74.0 1.4 copy-start.2
  74.0 2.1 copy-start
  74.0 77.5 %all-reduce.7.cloned.1.call-start = ((), (), s32[]{:S(2)}) async-start(), calls=%async_computation.17 | async-start | bytes 131072 | tf_op jit(solution)/shard_map/psum | solution.py:56
  76.1 34.2 %copy-start.4 = (bf16[6,1024,128]{2,1,0:T(8,128)(2,1)S(1)}, bf16[6,1024,128]{2,1,0:T(8,128)(2,1)}, u32[]{:S(2)}) copy-start(bf16[6,1024,128]{2,1,0:T(8,128)(2,1)} %param.46) | copy-start | bytes 4718596
  110.2 70.6 %all-gather.20.cloned.1.call-start = ((), (), s32[]{:S(2)}) async-start(), calls=%async_computation.28 | async-start | bytes 1310720 | tf_op jit(solution)/shard_map/all_gather | solution.py:34
  154.2 97.6 %reduce-scatter.11.cloned.1.call-start = ((), (), s32[]{:S(2)}) async-start(), calls=%async_computation.18 | async-start | bytes 2359296 | tf_op jit(solution)/shard_map/reduce_scatter | solution.py:36
  217.6 0.7 copy-start.14
  217.6 77.3 %all-reduce.13.cloned.1.call-start = ((), (), s32[]{:S(2)}) async-start(), calls=%async_computation.35 | async-start | bytes 131072 | tf_op jit(solution)/shard_map/psum | solution.py:56
  253.7 69.8 %all-gather.22.cloned.1.call-start = ((), (), s32[]{:S(2)}) async-start(), calls=%async_computation.29 | async-start | bytes 1310720 | tf_op jit(solution)/shard_map/all_gather | solution.py:34
  296.9 97.6 %reduce-scatter.13.cloned.1.call-start = ((), (), s32[]{:S(2)}) async-start(), calls=%async_computation.19 | async-start | bytes 2359296 | tf_op jit(solution)/shard_map/reduce_scatter | solution.py:36
  360.3 76.7 %all-gather.24.cloned.1.call-start = ((), (), s32[]{:S(2)}) async-start(), calls=%async_computation.30 | async-start | bytes 1310720 | tf_op jit(solution)/shard_map/all_gather | solution.py:34
  413.9 94.0 %reduce-scatter.15.cloned.1.call-start = ((), (), s32[]{:S(2)}) async-start(), calls=%async_computation.20 | async-start | bytes 2359296 | tf_op jit(solution)/shard_map/reduce_scatter | solution.py:36
  473.8 61.0 %all-gather.16.cloned.1.call-start = ((), (), s32[]{:S(2)}) async-start(), calls=%async_computation.21 | async-start | bytes 1310720 | tf_op jit(solution)/shard_map/all_gather | solution.py:73
  508.0 97.2 %reduce-scatter.17.cloned.1.call-start = ((), (), s32[]{:S(2)}) async-start(), calls=%async_computation.22 | async-start | bytes 2359296 | tf_op jit(solution)/shard_map/reduce_scatter | solution.py:75
  570.9 0.7 copy-start.13
  570.9 1.4 copy-start.3
  570.9 2.1 copy-start.1
  571.0 77.4 %all-reduce.9.cloned.1.call-start = ((), (), s32[]{:S(2)}) async-start(), calls=%async_computation.23 | async-start | bytes 131072 | tf_op jit(solution)/shard_map/psum | solution.py:94
  573.1 34.2 %copy-start.5 = (bf16[6,1024,128]{2,1,0:T(8,128)(2,1)S(1)}, bf16[6,1024,128]{2,1,0:T(8,128)(2,1)}, u32[]{:S(2)}) copy-start(bf16[6,1024,128]{2,1,0:T(8,128)(2,1)} %param.48) | copy-start | bytes 4718596
  573.1 75.3 %copy-start.9 = (bf16[128,1024]{1,0:T(8,128)(2,1)S(1)}, bf16[128,1024]{1,0:T(8,128)(2,1)}, u32[]{:S(2)}) copy-start(bf16[128,1024]{1,0:T(8,128)(2,1)} %reduce-scatter.11.cloned.1.call-done) | copy-start | bytes 786436
  573.1 75.3 %copy-start.10 = (bf16[128,1024]{1,0:T(8,128)(2,1)S(1)}, bf16[128,1024]{1,0:T(8,128)(2,1)}, u32[]{:S(2)}) copy-start(bf16[128,1024]{1,0:T(8,128)(2,1)} %reduce-scatter.13.cloned.1.call-done) | copy-start | bytes 786436
  573.1 75.3 %copy-start.11 = (bf16[128,1024]{1,0:T(8,128)(2,1)S(1)}, bf16[128,1024]{1,0:T(8,128)(2,1)}, u32[]{:S(2)}) copy-start(bf16[128,1024]{1,0:T(8,128)(2,1)} %reduce-scatter.9.cloned.1.call-done) | copy-start | bytes 786436
  607.2 70.0 %all-gather.26.cloned.1.call-start = ((), (), s32[]{:S(2)}) async-start(), calls=%async_computation.31 | async-start | bytes 1310720 | tf_op jit(solution)/shard_map/all_gather | solution.py:73
  650.5 97.6 %reduce-scatter.19.cloned.1.call-start = ((), (), s32[]{:S(2)}) async-start(), calls=%async_computation.24 | async-start | bytes 2359296 | tf_op jit(solution)/shard_map/reduce_scatter | solution.py:75
  713.9 0.7 copy-start.12
  713.9 77.3 %all-reduce.11.cloned.1.call-start = ((), (), s32[]{:S(2)}) async-start(), calls=%async_computation.34 | async-start | bytes 131072 | tf_op jit(solution)/shard_map/psum | solution.py:92
  750.1 69.8 %all-gather.28.cloned.1.call-start = ((), (), s32[]{:S(2)}) async-start(), calls=%async_computation.32 | async-start | bytes 1310720 | tf_op jit(solution)/shard_map/all_gather | solution.py:73
  793.2 97.6 %reduce-scatter.21.cloned.1.call-start = ((), (), s32[]{:S(2)}) async-start(), calls=%async_computation.25 | async-start | bytes 2359296 | tf_op jit(solution)/shard_map/reduce_scatter | solution.py:75
  856.6 76.6 %all-gather.30.cloned.1.call-start = ((), (), s32[]{:S(2)}) async-start(), calls=%async_computation.33 | async-start | bytes 1310720 | tf_op jit(solution)/shard_map/all_gather | solution.py:73
  910.1 94.0 %reduce-scatter.23.cloned.1.call-start = ((), (), s32[]{:S(2)}) async-start(), calls=%async_computation.26 | async-start | bytes 2359296 | tf_op jit(solution)/shard_map/reduce_scatter | solution.py:75
  969.9 34.2 %copy-start.6 = (bf16[128,1024]{1,0:T(8,128)(2,1)S(1)}, bf16[128,1024]{1,0:T(8,128)(2,1)}, u32[]{:S(2)}) copy-start(bf16[128,1024]{1,0:T(8,128)(2,1)} %reduce-scatter.19.cloned.1.call-done) | copy-start | bytes 786436
  969.9 34.2 %copy-start.7 = (bf16[128,1024]{1,0:T(8,128)(2,1)S(1)}, bf16[128,1024]{1,0:T(8,128)(2,1)}, u32[]{:S(2)}) copy-start(bf16[128,1024]{1,0:T(8,128)(2,1)} %reduce-scatter.21.cloned.1.call-done) | copy-start | bytes 786436
  969.9 34.2 %copy-start.8 = (bf16[128,1024]{1,0:T(8,128)(2,1)S(1)}, bf16[128,1024]{1,0:T(8,128)(2,1)}, u32[]{:S(2)}) copy-start(bf16[128,1024]{1,0:T(8,128)(2,1)} %reduce-scatter.17.cloned.1.call-done) | copy-start | bytes 786436
Sparse Core Ops, SparseCore 0:
  9.2 29.2 all-gather.17
  74.1 34.0 reduce-scatter.8
  111.1 40.3 all-reduce.6
  154.3 26.4 all-gather.19
  217.7 34.0 reduce-scatter.10
  254.5 40.4 all-reduce.12
  297.0 26.4 all-gather.21
  360.4 34.0 reduce-scatter.12
  414.1 22.9 all-gather.23
  473.9 34.0 reduce-scatter.14
  509.8 24.9 all-gather.15
  571.1 34.0 reduce-scatter.16
  608.0 40.3 all-reduce.8
  650.7 26.4 all-gather.25
  714.1 34.0 reduce-scatter.18
  750.8 40.3 all-reduce.10
  793.3 26.4 all-gather.27
  856.8 34.0 reduce-scatter.20
  910.3 22.8 all-gather.29
  970.1 34.0 reduce-scatter.22
where the time goes:
time: 1020 us; the launch traced here: 1010 us
  waiting for transfers between devices  596 us (58%)
  blocking collectives  313 us (31%)
  matrix products  47.9 us (5%)
  local copies, waits for them, and re-layouts  38.9 us (4%)
  between operations  14.7 us (1%)
    all_to_all x8, blocking collectives, shards(): lax.all_to_all(whole, 'row', split_axis=1, concat_axis=0, tiled=True)  248 us
    all_gather x8, waiting for transfers between devices, shards(): whole = lax.all_gather(rounded, 'col', axis=1, tiled=True)  209 us
    reduce_scatter x4, waiting for transfers between devices, shards(): lax.psum_scatter(sum_terms(moved, inv_upper[section]).astype(jnp.bfloat16...  130 us
    reduce_scatter x4, waiting for transfers between devices, shards(): lax.psum_scatter(sum_terms(moved, inv_lower[section]).astype(jnp.bfloat16...  129 us
    psum x2, waiting for transfers between devices, shards(): lax.psum(projections[1:].astype(jnp.bfloat16), 'col').astype(jnp.float32)  63.3 us
    psum x1, waiting for transfers between devices, shards(): lax.psum(projections[-1:].astype(jnp.bfloat16), 'col').astype(jnp.float32)  39 us
    psum x2, blocking collectives, shards(): lax.psum(projections[-1:].astype(jnp.bfloat16), 'col').astype(jnp.float32)  32.5 us
    psum x2, blocking collectives, shards(): lax.psum(projections[:1].astype(jnp.bfloat16), 'col').astype(jnp.float32)  32.4 us
  transfers between devices with their start and end apart: 20, of which 20 were waited for; matrix products, arithmetic and copies ran while one was open for 1% of the time, Pallas kernels for 0%

commit v1 on v0

--- a/solution.py
+++ b/solution.py
@@ -1,7 +1,11 @@
+import functools
+
 import jax
 import jax.numpy as jnp
 import numpy as np
 from jax import lax
+from jax.experimental import pallas as pl
+from jax.experimental.pallas import tpu as pltpu
 from jax.sharding import PartitionSpec as P
 
 RBLK = 32
@@ -107,6 +111,313 @@
     return jnp.stack(solutions)
 
 
+MESH = pl.DeviceIdType.MESH
+STREAMS = 4
+LAG = {"start": 0, "spread": 1, "multiply": 2, "reduce": 3, "finish": 5}
+PERIOD = 6
+
+
+def schedule(streams):
+    order = []
+    for stream in range(streams):
+        for stage, lag in LAG.items():
+            at = lag + stream * PERIOD / streams
+            late = int(at // PERIOD)
+            order.append((at - late * PERIOD, -late, stream, stage))
+    return sorted(order)
+
+
+def kernel(
+    shape, rhs, low_left, low_right, up_left, up_right, masks, inv_lower, inv_upper, out,
+    inv, left, right, source, moved, own, other, landed, chunks, arrived, proj, proj_in,
+    load_sem, g1_send, g1_recv, g2_send, g2_recv, d_send, d_recv, r_send, r_recv, p_send, p_recv,
+):
+    tiles, rows, cols, chips, streams, part = shape
+    pairs = low_left.shape[0]
+    per_col = rows // cols
+    lanes = inv_lower.shape[2]
+    piece = lanes // cols
+    row, col = lax.axis_index("row"), lax.axis_index("col")
+    chip, core = lax.div(row, 2), lax.rem(row, 2)
+    home = lax.div(row, per_col)
+
+    loads = [(rhs, out)]
+    loads += [(inv_lower.at[k], inv.at[k]) for k in range(tiles)]
+    loads += [(low_right, right.at[pl.ds(0, pairs)]), (low_left, left.at[pl.ds(0, pairs)])]
+    loads += [(up_right, right.at[pl.ds(pairs, pairs)]), (up_left, left.at[pl.ds(pairs, pairs)])]
+    loads += [(inv_upper.at[k], inv.at[2 * tiles - 1 - k]) for k in range(tiles - 1, -1, -1)]
+    slots = [0] + list(range(1, 1 + tiles)) + [2 * tiles + 1 + k for k in range(4)]
+    slots += list(range(1 + tiles, 1 + 2 * tiles))
+    copies = [pltpu.make_async_copy(a, b, load_sem.at[s]) for (a, b), s in zip(loads, slots)]
+    for copy in copies:
+        copy.start()
+    proj[...] = jnp.zeros_like(proj)
+    copies[0].wait()
+
+    def remote(src, dst, send, recv, to_row, to_col):
+        return pltpu.make_async_remote_copy(
+            src_ref=src, dst_ref=dst, send_sem=send, recv_sem=recv,
+            device_id=(to_row, to_col), device_id_type=MESH,
+        )
+
+    def own_lanes():
+        return pl.ds(pl.multiple_of(col * piece, piece), piece)
+
+    def geometry(step):
+        back = lax.div(step, tiles)
+        section = step + back * (2 * tiles - 1 - 2 * step)
+        count = (1 - back) * (tiles - 1 - section) + back * section
+        return back, section, count
+
+    def tile_of(back, section, u):
+        tile = (1 - back) * (section + 1) + u
+        pair = (1 - back) * (lax.div(tile * (tile + 2 * tiles - 1), 2) - tile * tiles + section)
+        pair = pair + back * (pairs + lax.div(section * (section + 2 * tiles - 1), 2) - section * tiles + u)
+        return tile, pair
+
+    def place(stream):
+        return pl.ds(stream * part, part)
+
+    def g1(step, stream, half, q):
+        side = lax.rem(step, 2)
+        return remote(
+            source.at[stream, :, pl.ds(half * lanes + q * piece, piece)],
+            moved.at[side, stream, core, chip, :, pl.ds(q * piece, piece)],
+            g1_send.at[stream, half * cols + q],
+            g1_recv.at[stream, side, row],
+            col * per_col + half,
+            q,
+        )
+
+    def g1_mine(half, q):
+        return jnp.logical_and(row == col * per_col + half, col == q)
+
+    def g2(step, stream, hop):
+        side = lax.rem(step, 2)
+        view = moved.at[side, stream, :, :, :, own_lanes()]
+        return remote(
+            view, view, g2_send.at[stream, hop], g2_recv.at[stream, side, hop],
+            row, lax.rem(col + hop, cols),
+        )
+
+    def swap(step, stream):
+        side = lax.rem(step, 2)
+        return remote(
+            other.at[stream], landed.at[side, stream], d_send.at[stream], d_recv.at[stream, side],
+            row + 1 - 2 * core, col,
+        )
+
+    def scatter(step, stream, hop):
+        side = lax.rem(step, 2)
+        to = lax.rem(chip + hop, chips)
+        return remote(
+            chunks.at[stream, to], arrived.at[side, stream, hop],
+            r_send.at[stream, hop], r_recv.at[stream, side, hop],
+            2 * to + core, col,
+        )
+
+    def project(step, stream, hop):
+        side = lax.rem(step, 2)
+        return remote(
+            proj.at[stream], proj_in.at[side, stream, hop],
+            p_send.at[stream, hop], p_recv.at[stream, side, hop],
+            row, lax.rem(col + hop, cols),
+        )
+
+    def update(step, stream):
+        back, section, count = geometry(step)
+        side = lax.rem(step, 2)
+        for hop in range(1, cols):
+            project(step, stream, hop).wait()
+
+        def one(u, carry):
+            tile, pair = tile_of(back, section, u)
+            total = proj[stream, u].astype(jnp.float32)
+            for hop in range(1, cols):
+                total += proj_in[side, stream, hop, u].astype(jnp.float32)
+            masked = (total * masks[pair]).astype(jnp.bfloat16)
+            out[tile, place(stream), :] -= times_inverse(masked, left[pair])
+            return carry
+
+        lax.fori_loop(0, count, one, 0)
+
+    def start(step, stream):
+        @pl.when(jnp.logical_and(step > 0, step != tiles))
+        def _():
+            update(step - 1, stream)
+
+        _, section, _ = geometry(step)
+        source[stream] = out[section, place(stream), :].astype(jnp.bfloat16)
+        for half in range(per_col):
+            for q in range(cols):
+                copy = g1(step, stream, half, q)
+                mine = g1_mine(half, q)
+
+                @pl.when(jnp.logical_not(mine))
+                def _():
+                    copy.start()
+
+                @pl.when(mine)
+                def _():
+                    pltpu.make_async_copy(
+                        copy.src_ref, copy.dst_ref, g1_recv.at[stream, lax.rem(step, 2), row]
+                    ).start()
+
+    def spread(step, stream):
+        side = lax.rem(step, 2)
+        for k in range(rows):
+            view = moved.at[side, stream, k % 2, k // 2, :, own_lanes()]
+            pltpu.make_async_copy(view, view, g1_recv.at[stream, side, k]).wait()
+        for hop in range(1, cols):
+            g2(step, stream, hop).start()
+        for half in range(per_col):
+            for q in range(cols):
+
+                @pl.when(jnp.logical_not(g1_mine(half, q)))
+                def _():
+                    g1(step, stream, half, q).wait_send()
+
+    def multiply(step, stream):
+        side = lax.rem(step, 2)
+        if stream == 0:
+            pltpu.make_async_copy(inv_lower.at[0], inv.at[step], load_sem.at[1 + step]).wait()
+        for hop in range(1, cols):
+            view = moved.at[
+                side, stream, :, :, :,
+                pl.ds(pl.multiple_of(lax.rem(col + cols - hop, cols) * piece, piece), piece),
+            ]
+            pltpu.make_async_copy(view, view, g2_recv.at[stream, side, hop]).wait()
+        theirs = moved[side, stream, 1 - core].reshape(chips * part, lanes)
+        other[stream] = (
+            times_inverse(theirs, inv[step]).astype(jnp.bfloat16).reshape(chips, part, -1)
+        )
+        swap(step, stream).start()
+        ours = moved[side, stream, core].reshape(chips * part, lanes)
+        own[stream] = times_inverse(ours, inv[step]).reshape(chips, part, -1)
+        for hop in range(1, cols):
+            g2(step, stream, hop).wait_send()
+
+    def reduce(step, stream):
+        side = lax.rem(step, 2)
+        swap(step, stream).wait()
+        for hop in list(range(1, chips)):
+            to = lax.rem(chip + hop, chips)
+            chunks[stream, to] = (
+                own[stream, to] + landed[side, stream, to].astype(jnp.float32)
+            ).astype(jnp.bfloat16)
+            scatter(step, stream, hop).start()
+
+    def finish(step, stream):
+        side = lax.rem(step, 2)
+        back, section, count = geometry(step)
+        total = own[stream, chip] + landed[side, stream, chip].astype(jnp.float32)
+        for hop in range(1, chips):
+            scatter(step, stream, hop).wait()
+            total += arrived[side, stream, hop].astype(jnp.float32)
+        out[section, place(stream), :] = total
+        if stream == 0:
+
+            @pl.when(step == 0)
+            def _():
+                for k in range(1 + tiles, 5 + tiles):
+                    copies[k].wait()
+
+        @pl.when(count > 0)
+        def _():
+            rounded = out[section, place(stream), :].astype(jnp.bfloat16)
+
+            def one(u, carry):
+                _, pair = tile_of(back, section, u)
+                proj[stream, u] = jnp.dot(
+                    rounded, right[pair], preferred_element_type=jnp.float32
+                ).astype(jnp.bfloat16)
+                return carry
+
+            lax.fori_loop(0, count, one, 0)
+            for hop in range(1, cols):
+                project(step, stream, hop).start()
+
+    stages = {
+        "start": start, "spread": spread, "multiply": multiply, "reduce": reduce, "finish": finish,
+    }
+    steps = 2 * tiles
+    order = schedule(streams)
+    latest = -min(shift for _, shift, _, _ in order)
+
+    def body(turn, carry):
+        for _, shift, stream, stage in order:
+            step = turn + shift
+
+            @pl.when(jnp.logical_and(step >= 0, step < steps))
+            def _():
+                stages[stage](step, stream)
+
+        return carry
+
+    lax.fori_loop(0, steps + latest, body, 0)
+
+
+def fused(
+    rows, cols, streams, right_sides, low_left, low_right, up_left, up_right, low_ranks, up_ranks,
+    inv_lower, inv_upper,
+):
+    tiles, held, wide = right_sides.shape
+    pairs, _, rank_cols = low_left.shape
+    lanes = inv_lower.shape[2]
+    chips = rows // 2
+    part = held // streams
+    masks = rank_mask(
+        jnp.concatenate([low_ranks, up_ranks]), np.arange(2 * pairs), rank_cols
+    ).reshape(2 * pairs, 1, rank_cols)
+    half = jnp.bfloat16
+    dma = pltpu.SemaphoreType.DMA
+    scratch = [
+        pltpu.VMEM((2 * tiles, wide, lanes), half),
+        pltpu.VMEM((2 * pairs, wide, rank_cols), half),
+        pltpu.VMEM((2 * pairs, wide, rank_cols), half),
+        pltpu.VMEM((streams, part, wide), half),
+        pltpu.VMEM((2, streams, 2, chips, part, lanes), half),
+        pltpu.VMEM((streams, chips, part, wide), jnp.float32),
+        pltpu.VMEM((streams, chips, part, wide), half),
+        pltpu.VMEM((2, streams, chips, part, wide), half),
+        pltpu.VMEM((streams, chips, part, wide), half),
+        pltpu.VMEM((2, streams, chips, part, wide), half),
+        pltpu.VMEM((streams, tiles - 1, part, rank_cols), half),
+        pltpu.VMEM((2, streams, cols, tiles - 1, part, rank_cols), half),
+        dma((2 * tiles + 5,)),
+        dma((streams, rows)), dma((streams, 2, rows)),
+        dma((streams, cols)), dma((streams, 2, cols)),
+        dma((streams,)), dma((streams, 2)),
+        dma((streams, chips)), dma((streams, 2, chips)),
+        dma((streams, cols)), dma((streams, 2, cols)),
+    ]
+    anywhere = pl.BlockSpec(memory_space=pl.ANY)
+    vmem = pl.BlockSpec(memory_space=pltpu.VMEM)
+    return pl.pallas_call(
+        functools.partial(kernel, (tiles, rows, cols, chips, streams, part)),
+        out_shape=jax.ShapeDtypeStruct(right_sides.shape, jnp.float32),
+        in_specs=[anywhere] * 5 + [vmem] + [anywhere] * 2,
+        out_specs=vmem,
+        scratch_shapes=scratch,
+        compiler_params=pltpu.CompilerParams(
+            has_side_effects=True, vmem_limit_bytes=60 * 1024 * 1024
+        ),
+    )(right_sides, low_left, low_right, up_left, up_right, masks, inv_lower, inv_upper)
+
+
+def pick(mesh):
+    rows, cols = mesh.shape["row"], mesh.shape["col"]
+
+    def run(right_sides, *rest):
+        held, lanes = right_sides.shape[1], rest[-1].shape[2]
+        fits = rows % 2 == 0 and rows % cols == 0 and lanes % (128 * cols) == 0
+        if fits and held % (16 * STREAMS) == 0:
+            return fused(rows, cols, STREAMS, right_sides, *rest)
+        return shards(right_sides, *rest)
+
+    return run
+
+
 def solution(mesh):
     in_specs = (
         P(None, "row", "col"),
@@ -120,4 +431,4 @@
         P(None, "col", "row"),
     )
     out_specs = P(None, "row", "col")
-    return jax.shard_map(shards, mesh=mesh, in_specs=in_specs, out_specs=out_specs, check_vma=False)
+    return jax.shard_map(pick(mesh), mesh=mesh, in_specs=in_specs, out_specs=out_specs, check_vma=False)

time: 1020 us -> 375 us (0.37)
  waiting for transfers between devices: 596 us -> 0 us
  Pallas kernels: 0 us -> 370 us
  blocking collectives: 313 us -> 0 us
  matrix products: 47.9 us -> 0 us
  local copies, waits for them, and re-layouts: 38.9 us -> 3.82 us
  between operations: 14.7 us -> 0.01 us
    pallas_call x0 -> x1, Pallas kernels: none -> 370 us  [fused(): pl.pallas_call(functools.partial(kernel, (tiles, rows, cols, chips, strea...]
    reduce_scatter x8 -> x0, waiting for transfers between devices: 260 us -> none  [the longest x4 130 us: shards(): lax.psum_scatter(sum_terms(moved, inv_upper[section]).astype(jnp.bfloat16...]
    all_to_all x8 -> x0, blocking collectives: 248 us -> none  [shards(): lax.all_to_all(whole, 'row', split_axis=1, concat_axis=0, tiled=True)]
    all_gather x8 -> x0, waiting for transfers between devices: 209 us -> none  [shards(): whole = lax.all_gather(rounded, 'col', axis=1, tiled=True)]
    psum x4 -> x0, waiting for transfers between devices: 126 us -> none  [the longest x2 63.3 us: shards(): lax.psum(projections[1:].astype(jnp.bfloat16), 'col').astype(jnp.float32)]
    psum x4 -> x0, blocking collectives: 64.9 us -> none  [the longest x2 32.5 us: shards(): lax.psum(projections[-1:].astype(jnp.bfloat16), 'col').astype(jnp.float32)]
    dot_general x20 -> x0, matrix products: 47.9 us -> none  [the longest x8 30.6 us: times_inverse(): lax.dot_general(block, inverse, (((1,), (1,)), ((), ())), preferred_eleme...]
    unnamed x39 -> x1, local copies, waits for them, and re-layouts: 14.4 us -> 3.16 us
  transfers between devices with their start and end apart: 20 -> 0, of which waited for: 20 -> 0; matrix products, arithmetic and copies ran while one was open for 1% -> 0% of each run, Pallas kernels for 0% -> 0%
where the time goes in v1:
time: 375 us
  Pallas kernels  370 us (99%)
  local copies, waits for them, and re-layouts  3.82 us (1%)
    pallas_call x1, Pallas kernels, fused(): pl.pallas_call(functools.partial(kernel, (tiles, rows, cols, chips, strea...  370 us

profile of v1, /device:TPU:0, one launch (start us, length us, event | category | flops | bytes accessed | tf_op | source)
XLA Modules:
  0.0 374.8 jit_solution(1508261775393809196)
XLA Ops:
  0.0 0.7 pad_add_fusion
  0.8 0.7 gather_fusion
  1.4 0.7 compare_convert_fusion.masks
  2.1 369.5 %shard_map.109 = f32[4,128,1024]{2,1,0:T(8,128)} custom-call(f32[4,128,1024]{2,1,0:T(8,128)} %rhs.1, bf16[6,1024,128]{2,1,0:T(8,128)(2,1)} %low_left.1, bf16[6,1024,128]{2,1,0:T(8,128)(2,1)} %low_right.1, bf16[6,1024,128]{2,1,0:T(8,128)(2,1)} %up_left.1, bf16[6,1024,128]{2,1,0:T(8,128)(2,1)} %up_right.1, f32[12,1,128]{2,1,0:T(1,128)} %compare_convert_fusion.masks, ...), custom_call_target="tpu_custom_call" | custom-call | tf_op jit(solution)/shard_map/pallas_call | solution.py:396
  371.6 3.2 copy.13
  (3 shorter events, 0.0 us)

commit v2 on v1

--- a/solution.py
+++ b/solution.py
@@ -113,8 +113,8 @@
 
 MESH = pl.DeviceIdType.MESH
 STREAMS = 4
-LAG = {"start": 0, "spread": 1, "multiply": 2, "reduce": 3, "finish": 5}
-PERIOD = 6
+LAG = {"start": 0, "spread": 0.7, "multiply": 1.4, "reduce": 1.65, "relay": 2.6, "finish": 3.5}
+PERIOD = 4
 
 
 def schedule(streams):
@@ -139,7 +139,7 @@
     piece = lanes // cols
     row, col = lax.axis_index("row"), lax.axis_index("col")
     chip, core = lax.div(row, 2), lax.rem(row, 2)
-    home = lax.div(row, per_col)
+    pair_at, member, pair_count = lax.div(chip, 2), lax.rem(chip, 2), chips // 2
 
     loads = [(rhs, out)]
     loads += [(inv_lower.at[k], inv.at[k]) for k in range(tiles)]
@@ -207,14 +207,22 @@
             row + 1 - 2 * core, col,
         )
 
-    def scatter(step, stream, hop):
-        side = lax.rem(step, 2)
-        to = lax.rem(chip + hop, chips)
+    def pass_on(step, stream, slot, to):
+        side = lax.rem(step, 2)
         return remote(
-            chunks.at[stream, to], arrived.at[side, stream, hop],
-            r_send.at[stream, hop], r_recv.at[stream, side, hop],
+            chunks.at[stream, slot], arrived.at[side, stream, slot],
+            r_send.at[stream, slot], r_recv.at[stream, side, slot],
             2 * to + core, col,
         )
+
+    def pair_copy(step, stream, hop):
+        return pass_on(step, stream, hop, chip + 1 - 2 * member)
+
+    def relay_copy(step, stream, hop):
+        return pass_on(step, stream, pair_count + hop, 2 * lax.rem(pair_at + hop, pair_count) + member)
+
+    def held_sum(step, stream, to):
+        return own[stream, to] + landed[lax.rem(step, 2), stream, to].astype(jnp.float32)
 
     def project(step, stream, hop):
         side = lax.rem(step, 2)
@@ -298,22 +306,30 @@
             g2(step, stream, hop).wait_send()
 
     def reduce(step, stream):
-        side = lax.rem(step, 2)
         swap(step, stream).wait()
-        for hop in list(range(1, chips)):
-            to = lax.rem(chip + hop, chips)
-            chunks[stream, to] = (
-                own[stream, to] + landed[side, stream, to].astype(jnp.float32)
-            ).astype(jnp.bfloat16)
-            scatter(step, stream, hop).start()
+        for hop in list(range(1, pair_count)) + [0]:
+            to = 2 * lax.rem(pair_at + hop, pair_count) + 1 - member
+            chunks[stream, hop] = held_sum(step, stream, to).astype(jnp.bfloat16)
+            pair_copy(step, stream, hop).start()
+
+    def relay(step, stream):
+        side = lax.rem(step, 2)
+        for hop in range(1, pair_count):
+            pair_copy(step, stream, hop).wait()
+            to = 2 * lax.rem(pair_at + hop, pair_count) + member
+            total = held_sum(step, stream, to) + arrived[side, stream, hop].astype(jnp.float32)
+            chunks[stream, pair_count + hop] = total.astype(jnp.bfloat16)
+            relay_copy(step, stream, hop).start()
 
     def finish(step, stream):
         side = lax.rem(step, 2)
         back, section, count = geometry(step)
-        total = own[stream, chip] + landed[side, stream, chip].astype(jnp.float32)
-        for hop in range(1, chips):
-            scatter(step, stream, hop).wait()
-            total += arrived[side, stream, hop].astype(jnp.float32)
+        total = held_sum(step, stream, chip)
+        pair_copy(step, stream, 0).wait()
+        total += arrived[side, stream, 0].astype(jnp.float32)
+        for hop in range(1, pair_count):
+            relay_copy(step, stream, hop).wait()
+            total += arrived[side, stream, pair_count + hop].astype(jnp.float32)
         out[section, place(stream), :] = total
         if stream == 0:
 
@@ -338,7 +354,8 @@
                 project(step, stream, hop).start()
 
     stages = {
-        "start": start, "spread": spread, "multiply": multiply, "reduce": reduce, "finish": finish,
+        "start": start, "spread": spread, "multiply": multiply, "reduce": reduce, "relay": relay,
+        "finish": finish,
     }
     steps = 2 * tiles
     order = schedule(streams)
@@ -410,7 +427,7 @@
 
     def run(right_sides, *rest):
         held, lanes = right_sides.shape[1], rest[-1].shape[2]
-        fits = rows % 2 == 0 and rows % cols == 0 and lanes % (128 * cols) == 0
+        fits = rows % 4 == 0 and rows % cols == 0 and lanes % (128 * cols) == 0
         if fits and held % (16 * STREAMS) == 0:
             return fused(rows, cols, STREAMS, right_sides, *rest)
         return shards(right_sides, *rest)

time: 375 us -> 305 us (0.81)
  Pallas kernels: 370 us -> 299 us
    pallas_call x1, Pallas kernels: 370 us -> 299 us  [fused(): pl.pallas_call(functools.partial(kernel, (tiles, rows, cols, chips, strea...]
where the time goes in v2:
time: 305 us; the launch traced here: 304 us
  Pallas kernels  299 us (98%)
  local copies, waits for them, and re-layouts  3.82 us (1%)
    pallas_call x1, Pallas kernels, fused(): pl.pallas_call(functools.partial(kernel, (tiles, rows, cols, chips, strea...  299 us

profile of v2, /device:TPU:0, one launch (start us, length us, event | category | flops | bytes accessed | tf_op | source)
XLA Modules:
  0.0 304.3 jit_solution(13526217055980984246)
XLA Ops:
  0.0 0.7 pad_add_fusion
  0.8 0.7 gather_fusion
  1.4 0.7 compare_convert_fusion.masks
  2.1 299.1 %shard_map.109 = f32[4,128,1024]{2,1,0:T(8,128)} custom-call(f32[4,128,1024]{2,1,0:T(8,128)} %rhs.1, bf16[6,1024,128]{2,1,0:T(8,128)(2,1)} %low_left.1, bf16[6,1024,128]{2,1,0:T(8,128)(2,1)} %low_right.1, bf16[6,1024,128]{2,1,0:T(8,128)(2,1)} %up_left.1, bf16[6,1024,128]{2,1,0:T(8,128)(2,1)} %up_right.1, f32[12,1,128]{2,1,0:T(1,128)} %compare_convert_fusion.masks, ...), custom_call_target="tpu_custom_call" | custom-call | tf_op jit(solution)/shard_map/pallas_call | solution.py:413
  301.2 3.2 %copy.13 = f32[4,128,1024]{2,1,0:T(8,128)} copy(f32[4,128,1024]{2,1,0:T(8,128)} %shard_map.109) | data formatting | bytes 4194304
  (3 shorter events, 0.0 us)
